TPU v7x, 32 devices: a whole 2x2x4 slice. The times are simulated.
32 devices in a mesh: dp: 2 (over x), vp: 4 (over z), tp: 4 (over y, core).
Axes of the slice: x: 2, y: 2, z: 4, core: 2. Of those that a mesh axis runs over, the one named last changes fastest.
Arguments:
- hidden: bfloat16 [128, 1536], P('dp', 'tp'), parts along dimension 0
- lnf_gain: float32 [1536], P('tp')
- lnf_bias: float32 [1536], P('tp')
- emb_table: bfloat16 [250880, 1536], P('vp', 'tp')
- next_tok: int32 [128], P('dp'), parts along dimension 0
- eln_gain: float32 [1536], P('tp')
- eln_bias: float32 [1536], P('tp')
Outputs:
- output 1: float32 [128, 250880], P('dp', ('vp', 'tp')), parts along dimension 0
- output 2: float32 [128], P('dp'), parts along dimension 0
- output 3: bfloat16 [128, 1536], P('dp', 'tp'), parts along dimension 0
There are 2 independent parts. A program takes and returns all parts, laid end to end along the dimension named above; an argument that names none is the same for every part.
All inputs are finite; a program needn't handle non-finite values.
Results may differ from a plain program's by a relative error of at most 0.001.
Values sent between devices are 32-bit elements.
A program may use at most 1 GiB of HBM per device.

v0:
```python
import jax
import jax.numpy as jnp
from jax import lax
from jax.sharding import PartitionSpec as P

NORM_EPS = 1e-5


def norm_shard(rows_in, norm_gain, norm_bias, full_width):
    rows_f32 = rows_in.astype(jnp.float32)
    row_sums = jnp.stack([jnp.sum(rows_f32, axis=1), jnp.sum(rows_f32 * rows_f32, axis=1)])
    row_sums = lax.psum(row_sums, "tp")
    row_mean = row_sums[0] / full_width
    row_var = row_sums[1] / full_width - row_mean * row_mean
    scaled = (rows_f32 - row_mean[:, None]) * lax.rsqrt(row_var + NORM_EPS)[:, None]
    return (scaled * norm_gain + norm_bias).astype(jnp.bfloat16)


def global_lse(logits):
    row_top = lax.pmax(jnp.max(logits, axis=1), ("vp", "tp"))
    exp_total = lax.psum(jnp.sum(jnp.exp(logits - row_top[:, None]), axis=1), ("vp", "tp"))
    return row_top + jnp.log(exp_total)


def solution(mesh):
    tp_size = mesh.shape["tp"]

    def per_device(hidden, lnf_gain, lnf_bias, emb_table, next_tok, eln_gain, eln_bias):
        full_width = hidden.shape[1] * tp_size
        normed = norm_shard(hidden, lnf_gain, lnf_bias, full_width)
        shard_logits = lax.dot_general(normed, emb_table, (((1,), (1,)), ((), ())), preferred_element_type=jnp.float32)
        logits = lax.psum_scatter(shard_logits, "tp", scatter_dimension=1, tiled=True)
        log_sum = global_lse(logits)
        logprobs = logits - log_sum[:, None]
        block_rows = emb_table.shape[0]
        local_idx = next_tok - lax.axis_index("vp") * block_rows
        is_owned = (local_idx >= 0) & (local_idx < block_rows)
        picked = jnp.take(emb_table, jnp.clip(local_idx, 0, block_rows - 1), axis=0).astype(jnp.float32)
        picked = jnp.where(is_owned[:, None], picked, jnp.zeros_like(picked))
        tok_rows = lax.psum(picked, "vp")
        next_in = norm_shard(tok_rows, eln_gain, eln_bias, full_width)
        return logprobs, log_sum, next_in

    return jax.shard_map(
        per_device,
        mesh=mesh,
        in_specs=(P("dp", "tp"), P("tp"), P("tp"), P("vp", "tp"), P("dp"), P("tp"), P("tp")),
        out_specs=(P("dp", ("vp", "tp")), P("dp"), P("dp", "tp")),
        check_vma=False,
    )
```

profile of v0, /device:TPU:0, one launch (start us, length us, event | category | flops | bytes accessed | tf_op | source)
XLA Modules:
  0.0 394.2 jit_solution(11997480901558072006)
XLA Ops:
  7.2 0.0 all-reduce.3.cloned.1.call-start
  7.2 0.7 compare_and_fusion
  7.9 2.6 gather_fusion
  10.5 0.7 convert_select_fusion
  11.3 0.0 all-reduce.3.cloned.1.call-update
  11.3 0.0 reduce-scatter.4.cloned.1.call-start
  11.3 0.9 convert_reduce_fusion
  12.3 37.1 %all-reduce.3.cloned.1.call-done = f32[64,384]{1,0:T(8,128)} async-done(((f32[64,384]{1,0:T(8,128)}), f32[64,384]{1,0:T(8,128)}) %all-reduce.3.cloned.1.call-update) | async-done | bytes 98320 | tf_op jit(solution)/shard_map/psum | solution.py:40
  49.4 1.0 fusion.14
  50.4 5.7 %all-reduce = (f32[2,64]{1,0:T(2,128)S(1)}, f32[2,64]{1,0:T(2,128)S(1)}) all-reduce(f32[2,64]{1,0:T(2,128)S(1)} %get-tuple-element.12, f32[2,64]{1,0:T(2,128)S(1)} %get-tuple-element.13), channel_id=1, replica_groups=mesh['dp'=2,'vp'=4,'tp'=4] {'tp'}, use_global_device_ids=true, to_apply=%region_2.0 | all-reduce | flops 256 | bytes 2048 | tf_op jit(solution)/shard_map/psum | solution.py:12
  56.1 28.0 %convolution_bitcast_fusion = f32[62720,64]{1,0:T(8,128)} fusion(bf16[62720,384]{1,0:T(8,128)(2,1)} %param.10, bf16[64,384]{1,0:T(8,128)(2,1)} %param.7, f32[384]{0:T(512)} %param.9, f32[384]{0:T(512)} %param.8, f32[64]{0:T(128)S(1)} %fusion.13, f32[64]{0:T(128)S(1)} %multiply_bitcast_fusion.1), kind=kOutput, calls=%fused_computation.1 | convolution fusion | flops 3082960896 | bytes 64278016
  84.1 0.0 reduce-scatter.4.cloned.1.call-update
  84.2 0.8 copy-done
  85.0 0.0 copy-done.1
  85.0 0.0 copy-done.2
  85.0 0.7 add_convert_fusion
  85.7 221.8 %reduce-scatter.4.cloned.1.call-done = f32[15680,64]{1,0:T(8,128)} async-done(((f32[62720,64]{1,0:T(8,128)}), f32[15680,64]{1,0:T(8,128)}) %reduce-scatter.4.cloned.1.call-update) | async-done | bytes 4014096
  307.6 4.4 %bitcast_reduce_fusion = f32[64]{0:T(128)S(1)} fusion(f32[15680,64]{1,0:T(8,128)} %reduce-scatter.4.cloned.1.call-done), kind=kLoop, calls=%fused_computation.34 | loop fusion | flops 1003456 | bytes 4014336 | tf_op jit(solution)/shard_map/reduce_max | solution.py:20
  312.0 32.0 %pmax.7 = f32[64]{0:T(128)S(1)} all-reduce(f32[64]{0:T(128)S(1)} %bitcast_reduce_fusion), channel_id=1, replica_groups=mesh['dp'=2,'vp'=4,'tp'=4] {'vp','tp'}, use_global_device_ids=true, to_apply=%region_5.0 | all-reduce | flops 64 | bytes 512 | tf_op jit(solution)/shard_map/pmax | solution.py:20
  344.0 6.6 %copy.11 = f32[64,15680]{1,0:T(8,128)} copy(f32[64,15680]{0,1:T(8,128)} %bitcast.29) | data formatting | bytes 8028160
  350.6 2.8 exponential_reduce_fusion
  353.4 29.5 %psum.29 = f32[64]{0:T(128)S(1)} all-reduce(f32[64]{0:T(128)S(1)} %exponential_reduce_fusion), channel_id=1, replica_groups=mesh['dp'=2,'vp'=4,'tp'=4] {'vp','tp'}, use_global_device_ids=true, to_apply=%region_7.0 | all-reduce | flops 64 | bytes 512 | tf_op jit(solution)/shard_map/psum | solution.py:21
  382.9 4.4 %broadcast_subtract_fusion = f32[64,15680]{1,0:T(8,128)} fusion(f32[64,15680]{1,0:T(8,128)} %copy.11, f32[64]{0:T(128)S(1)} %log_add_fusion), kind=kLoop, calls=%fused_computation.3 | loop fusion | flops 1003520 | bytes 8028416 | tf_op jit(solution)/shard_map/sub | solution.py:34
  387.4 0.0 copy-done.3
  (11 shorter events, 0.1 us)
Async XLA Ops:
  7.2 42.2 %all-reduce.3.cloned.1.call-start = ((), (), s32[]{:S(2)}) async-start(), calls=%async_computation.1 | async-start | bytes 196608 | tf_op jit(solution)/shard_map/psum | solution.py:40
  11.3 296.3 %reduce-scatter.4.cloned.1.call-start = ((), (), s32[]{:S(2)}) async-start(), calls=%async_computation.2 | async-start | bytes 40140800
  84.1 0.9 copy-start
  84.1 0.9 copy-start.1
  84.1 0.9 copy-start.2
  382.9 4.4 %copy-start.3 = (f32[64]{0:T(128)}, f32[64]{0:T(128)S(1)}, u32[]{:S(2)}) copy-start(f32[64]{0:T(128)S(1)} %log_add_fusion) | copy-start | bytes 772
Sparse Core Ops, SparseCore 0:
  11.4 37.9 all-reduce.2
  84.3 223.2 reduce-scatter.3
where the time goes:
time: 394 us
  waiting for transfers between devices  259 us (66%)
  blocking collectives  67.1 us (17%)
  matrix products  28 us (7%)
  other arithmetic  15.7 us (4%)
  between operations  14.1 us (4%)
  local copies, waits for them, and re-layouts  10.1 us (3%)
    unnamed x3, waiting for transfers between devices  222 us
    psum x1, waiting for transfers between devices, per_device(): tok_rows = lax.psum(picked, 'vp')  37.1 us
    pmax x1, blocking collectives, global_lse(): row_top = lax.pmax(jnp.max(logits, axis=1), ('vp', 'tp'))  32 us
    psum x1, blocking collectives, global_lse(): lax.psum(jnp.sum(jnp.exp(logits - row_top[:, None]), axis=1), ('vp', 'tp'))  29.5 us
    unnamed x1, matrix products  28 us
  transfers between devices with their start and end apart: 2, of which 2 were waited for; matrix products, arithmetic and copies ran while one was open for 0% of the time, Pallas kernels for 0%

commit v1 on v0

v1 whole, which is shorter than its diff:
```python
import functools

import jax
import jax.numpy as jnp
from jax import lax
from jax.experimental import pallas as pl
from jax.experimental.pallas import tpu as pltpu
from jax.sharding import PartitionSpec as P

NORM_EPS = 1e-5
CHUNK = 1024
LANES = 128
DEPTH = 3
MESH = pl.DeviceIdType.MESH


def head_kernel(
    n_vp, n_full, rem, width,
    hid_hbm, gain1_hbm, bias1_hbm, tab_hbm, tok_hbm, gain2_hbm, bias2_hbm,
    logits, lse_out, next_out,
    hid, gain1, bias1, gain2, bias2, tok, tab, tab_rem, normed, picked, picked_rx,
    tx, rx, acc, y_rx, m_run, s_run, stat_slots, stat2_slots, lse_slots,
    in_sem, tab_sem, rem_sem, stat_send, stat_recv, stat2_send, stat2_recv,
    tx_send, tx_recv, y_send, y_recv, pick_send, pick_recv, lse_send, lse_recv,
):
    rows = hid.shape[0]
    n_chunks = n_full + 1
    seg = n_full * CHUNK + rem
    rem_pad = tab_rem.shape[1]
    vp = lax.axis_index("vp")
    tp = lax.axis_index("tp")
    chip_y = tp // 2
    core = lax.rem(tp, 2)
    sibling = tp + 1 - 2 * core
    across = lax.rem(tp + 2, 4)
    my_rank = vp * 4 + tp

    peers = []
    for dz in reversed(range(n_vp)):
        for dt in reversed(range(4)):
            if dz or dt:
                peers.append((dz, dt, dz * 4 + dt))

    def peer_id(dz, dt):
        return {"vp": lax.rem(vp + dz, n_vp), "tp": lax.rem(tp + dt, 4)}

    barrier = pltpu.get_barrier_semaphore()
    for dz, dt, _ in peers:
        pl.semaphore_signal(barrier, inc=1, device_id=peer_id(dz, dt), device_id_type=MESH)

    def seg_start(phase, which):
        y = chip_y + (1 - phase) * (1 - 2 * chip_y)
        c = core + (1 - which) * (1 - 2 * core)
        return (y * 2 + c) * seg

    def row_start(i, which):
        phase = jnp.where(i >= n_full, 1, 0)
        k = i - phase * n_full
        return pl.multiple_of(seg_start(phase, which) + k * CHUNK, 64)

    def tab_copy(i, which):
        slot = lax.rem(i, DEPTH)
        return pltpu.make_async_copy(
            tab_hbm.at[pl.ds(row_start(i, which), CHUNK), :], tab.at[slot, which], tab_sem.at[slot, which]
        )

    def rem_start(phase, which):
        return pl.multiple_of(seg_start(phase, which) + n_full * CHUNK, 64)

    def rem_copy(phase, which):
        return pltpu.make_async_copy(
            tab_hbm.at[pl.ds(rem_start(phase, which), rem), :],
            tab_rem.at[phase * 2 + which, pl.ds(0, rem), :],
            rem_sem.at[phase * 2 + which],
        )

    small = [
        pltpu.make_async_copy(hid_hbm, hid, in_sem.at[0]),
        pltpu.make_async_copy(gain1_hbm, gain1, in_sem.at[1]),
        pltpu.make_async_copy(bias1_hbm, bias1, in_sem.at[2]),
        pltpu.make_async_copy(gain2_hbm, gain2, in_sem.at[3]),
        pltpu.make_async_copy(bias2_hbm, bias2, in_sem.at[4]),
        pltpu.make_async_copy(tok_hbm, tok, in_sem.at[5]),
    ]
    for copy in small:
        copy.start()
    for i in range(min(DEPTH - 1, 2 * n_full)):
        for which in range(2):
            tab_copy(i, which).start()
    for phase in range(2):
        for which in range(2):
            rem_copy(phase, which).start()

    picked[...] = jnp.zeros_like(picked)
    m_run[...] = jnp.full_like(m_run, -jnp.inf)
    s_run[...] = jnp.zeros_like(s_run)
    empty = jnp.zeros((1, 8, LANES), jnp.float32)
    stat_slots[pl.ds(tp, 1)] = empty
    stat2_slots[pl.ds(tp, 1)] = empty
    lse_slots[pl.ds(my_rank, 1)] = empty
    tab_rem[:, rem:, :] = jnp.zeros((4, rem_pad - rem, width), jnp.bfloat16)

    lane = lax.broadcasted_iota(jnp.int32, (rows, LANES), 1)

    def stat_tile(x):
        s1 = jnp.sum(x, axis=1, keepdims=True)
        s2 = jnp.sum(x * x, axis=1, keepdims=True)
        both = jnp.where(lane == 0, s1, jnp.where(lane == 1, s2, 0.0))
        return both.T[:8, :]

    def stat_copy(slots, send, recv, d):
        return pltpu.make_async_remote_copy(
            src_ref=slots.at[tp], dst_ref=slots.at[tp], send_sem=send.at[d - 1], recv_sem=recv.at[d - 1],
            device_id=peer_id(0, d), device_id_type=MESH,
        )

    def norm(x, slots, send, recv, gain, bias):
        for d in (2, 3, 1):
            stat_copy(slots, send, recv, d).wait_recv()
        total = (slots[0] + slots[1]) + (slots[2] + slots[3])
        full_width = 4.0 * width
        mean = total[0:1, :] / full_width
        var = total[1:2, :] / full_width - mean * mean
        inv = lax.rsqrt(var + NORM_EPS)
        row = lax.broadcasted_iota(jnp.int32, (8, LANES), 0)
        back = jnp.where(row == 0, mean, inv).T
        mean_c = back[:rows, 0:1]
        inv_c = back[:rows, 1:2]
        return (x - mean_c) * inv_c * gain + bias

    small[0].wait()
    x1 = hid[...].astype(jnp.float32)
    stat_slots[pl.ds(tp, 1), :, 0:rows] = stat_tile(x1)[None]
    for copy in small[1:]:
        copy.wait()
    pl.semaphore_wait(barrier, len(peers))
    for d in (2, 3, 1):
        stat_copy(stat_slots, stat_send, stat_recv, d).start()
    normed[...] = norm(
        x1, stat_slots, stat_send, stat_recv, gain1[...].reshape(1, width), bias1[...].reshape(1, width)
    ).astype(jnp.bfloat16)

    def tx_copy(e, cols=None):
        view = (lambda r: r.at[e]) if cols is None else (lambda r: r.at[e, :, pl.ds(0, cols)])
        return pltpu.make_async_remote_copy(
            src_ref=view(tx), dst_ref=view(rx), send_sem=tx_send.at[e], recv_sem=tx_recv.at[e],
            device_id={"tp": sibling}, device_id_type=MESH,
        )

    def y_copy(e, cols=None):
        view = (lambda r: r.at[e]) if cols is None else (lambda r: r.at[e, :, pl.ds(0, cols)])
        return pltpu.make_async_remote_copy(
            src_ref=view(acc), dst_ref=view(y_rx), send_sem=y_send.at[e], recv_sem=y_recv.at[e],
            device_id={"tp": across}, device_id_type=MESH,
        )

    def partial(block):
        return lax.dot_general(
            normed[...], block, (((1,), (1,)), ((), ())), preferred_element_type=jnp.float32
        )

    tok_col = jnp.broadcast_to(tok[...], (8, rows)).T[:, 0:1]
    tok_local = tok_col - vp * (4 * seg)

    def add_picked(block, start):
        n = block.shape[0]
        at = lax.broadcasted_iota(jnp.int32, (rows, n), 1)
        hot = jnp.where(at == tok_local - start, 1.0, 0.0).astype(jnp.bfloat16)
        picked[...] += lax.dot_general(
            hot, block, (((1,), (0,)), ((), ())), preferred_element_type=jnp.float32
        )

    def run_phase(phase):
        base = phase * n_chunks

        def body(i, carry):
            k = i - phase * n_full
            e = base + k

            @pl.when(i + DEPTH - 1 < 2 * n_full)
            def _():
                tab_copy(i + DEPTH - 1, 0).start()
                tab_copy(i + DEPTH - 1, 1).start()

            slot = lax.rem(i, DEPTH)
            tab_copy(i, 0).wait()
            tx[e] = partial(tab[slot, 0])
            tab_copy(i, 1).wait()
            acc[e] = partial(tab[slot, 1])
            tx_copy(e).start()

            @pl.when(k > 0)
            def _():
                tx_copy(e - 1).wait_recv()
                acc[e - 1] = acc[e - 1] + rx[e - 1]

            add_picked(tab[slot, 0], row_start(i, 0))
            add_picked(tab[slot, 1], row_start(i, 1))
            if phase == 0:
                @pl.when(k > 0)
                def _():
                    y_copy(e - 1).start()
            return carry

        lax.fori_loop(phase * n_full, (phase + 1) * n_full, body, 0)
        last = base + n_full
        rem_copy(phase, 0).wait()
        tx[last, :, 0:rem_pad] = partial(tab_rem[phase * 2])
        rem_copy(phase, 1).wait()
        acc[last, :, 0:rem_pad] = partial(tab_rem[phase * 2 + 1])
        tx_copy(last, rem_pad).start()
        tx_copy(last - 1).wait_recv()
        acc[last - 1] = acc[last - 1] + rx[last - 1]
        for which in range(2):
            block = tab_rem[phase * 2 + which]
            at = lax.broadcasted_iota(jnp.int32, (rows, rem_pad), 1)
            hit = (at == tok_local - rem_start(phase, which)) & (at < rem)
            hot = jnp.where(hit, 1.0, 0.0).astype(jnp.bfloat16)
            picked[...] += lax.dot_general(
                hot, block, (((1,), (0,)), ((), ())), preferred_element_type=jnp.float32
            )
        if phase == 0:
            y_copy(last - 1).start()
        tx_copy(last, rem_pad).wait_recv()
        acc[last, :, 0:rem_pad] = acc[last, :, 0:rem_pad] + rx[last, :, 0:rem_pad]

    run_phase(0)
    y_copy(n_full, rem_pad).start()
    run_phase(1)

    def pick_copy(dz):
        return pltpu.make_async_remote_copy(
            src_ref=picked, dst_ref=picked_rx.at[vp], send_sem=pick_send.at[dz - 1], recv_sem=pick_recv.at[dz - 1],
            device_id=peer_id(dz, 0), device_id_type=MESH,
        )

    for dz in range(1, n_vp):
        pick_copy(dz).start()
    picked_rx[pl.ds(vp, 1)] = picked[...][None]
    for dz in range(1, n_vp):
        pick_copy(dz).wait_recv()
    x2 = picked_rx[0]
    for z in range(1, n_vp):
        x2 = x2 + picked_rx[z]
    stat2_slots[pl.ds(tp, 1), :, 0:rows] = stat_tile(x2)[None]
    for d in (2, 3, 1):
        stat_copy(stat2_slots, stat2_send, stat2_recv, d).start()
    next_out[...] = norm(
        x2, stat2_slots, stat2_send, stat2_recv, gain2[...].reshape(1, width), bias2[...].reshape(1, width)
    ).astype(jnp.bfloat16)

    def absorb(k, cols):
        e = n_chunks + k
        blocks = cols // LANES
        top = m_run[...]
        for b in range(blocks):
            sl = pl.ds(b * LANES, LANES)
            z = acc[e, :, sl] + y_rx[k, :, sl]
            logits[k, :, sl] = z
            if cols != CHUNK and (b + 1) * LANES > rem:
                z = jnp.where(lane < rem - b * LANES, z, -jnp.inf)
            top = jnp.maximum(top, z)
        total = s_run[...] * jnp.exp(m_run[...] - top)
        for b in range(blocks):
            z = logits[k, :, pl.ds(b * LANES, LANES)]
            if cols != CHUNK and (b + 1) * LANES > rem:
                z = jnp.where(lane < rem - b * LANES, z, -jnp.inf)
            total = total + jnp.exp(z - top)
        m_run[...] = top
        s_run[...] = total

    def absorb_body(k, carry):
        y_copy(k).wait_recv()
        absorb(k, CHUNK)
        return carry

    lax.fori_loop(0, n_full, absorb_body, 0)
    y_copy(n_full, rem_pad).wait_recv()
    absorb(n_full, rem_pad)

    m_t = m_run[...].T
    top = jnp.max(m_t, axis=0, keepdims=True)
    tot = jnp.sum(s_run[...].T * jnp.exp(m_t - top), axis=0, keepdims=True)
    row = lax.broadcasted_iota(jnp.int32, (8, rows), 0)
    lse_slots[pl.ds(my_rank, 1), :, 0:rows] = jnp.where(row == 0, top, tot)[None]

    def lse_copy(dz, dt, j):
        return pltpu.make_async_remote_copy(
            src_ref=lse_slots.at[my_rank], dst_ref=lse_slots.at[my_rank],
            send_sem=lse_send.at[j - 1], recv_sem=lse_recv.at[j - 1],
            device_id=peer_id(dz, dt), device_id_type=MESH,
        )

    for dz, dt, j in peers:
        lse_copy(dz, dt, j).start()

    def drain(e, carry):
        tx_copy(e).wait_send()
        tx_copy(n_chunks + e).wait_send()
        y_copy(e).wait_send()
        return carry

    lax.fori_loop(0, n_full, drain, 0)
    tx_copy(n_full, rem_pad).wait_send()
    tx_copy(n_chunks + n_full, rem_pad).wait_send()
    y_copy(n_full, rem_pad).wait_send()
    for d in (1, 2, 3):
        stat_copy(stat_slots, stat_send, stat_recv, d).wait_send()
        stat_copy(stat2_slots, stat2_send, stat2_recv, d).wait_send()
    for dz in range(1, n_vp):
        pick_copy(dz).wait_send()

    for dz, dt, j in peers:
        lse_copy(dz, dt, j).wait_recv()
    tops = [lse_slots[r, 0:1, :] for r in range(n_vp * 4)]
    top = functools.reduce(jnp.maximum, tops)
    tot = functools.reduce(
        jnp.add, [lse_slots[r, 1:2, :] * jnp.exp(tops[r] - top) for r in range(n_vp * 4)]
    )
    lse_out[...] = jnp.broadcast_to(top + jnp.log(tot), (8, LANES))
    for dz, dt, j in peers:
        lse_copy(dz, dt, j).wait_send()


def finish_kernel(n_full, rem, logits, lse, next_rows, out_hbm, sum_out, next_out, stage, sem):
    rows = stage.shape[0]
    log_sum = lse[...].T[:rows, 0:1]
    copies = []
    for r in range(rows // 8):
        here = slice(8 * r, 8 * r + 8)
        part = jnp.broadcast_to(log_sum[here], (8, LANES))
        for k in range(n_full + 1):
            cols = CHUNK if k < n_full else rem
            for b in range(0, cols, LANES):
                w = min(LANES, cols - b)
                at = k * CHUNK + b
                stage[here, at:at + w] = logits[k, here, b:b + w] - part[:, :w]
        copy = pltpu.make_async_copy(stage.at[here, :], out_hbm.at[here, :], sem.at[r])
        copy.start()
        copies.append(copy)
    sum_out[...] = lse[0:1, 0:rows]
    next_out[...] = next_rows[...]
    for copy in copies:
        copy.wait()


def solution(mesh):
    n_vp = mesh.shape["vp"]
    assert mesh.shape["tp"] == 4

    def per_device(hidden, lnf_gain, lnf_bias, emb_table, next_tok, eln_gain, eln_bias):
        rows, width = hidden.shape
        seg = emb_table.shape[0] // 4
        n_full, rem = divmod(seg, CHUNK)
        n_chunks = n_full + 1
        rem_pad = -(-rem // LANES) * LANES
        f32, bf16 = jnp.float32, jnp.bfloat16
        dma = pltpu.SemaphoreType.DMA
        hbm = pl.BlockSpec(memory_space=pltpu.HBM)
        vmem = pl.BlockSpec(memory_space=pltpu.VMEM)
        big = (64 * 1024 * 1024)
        logits, lse, next_rows = pl.pallas_call(
            functools.partial(head_kernel, n_vp, n_full, rem, width),
            out_shape=(
                pltpu.VMEM((n_chunks, rows, CHUNK), f32),
                pltpu.VMEM((8, LANES), f32),
                pltpu.VMEM((rows, width), bf16),
            ),
            in_specs=[hbm] * 7,
            out_specs=(vmem, vmem, vmem),
            scratch_shapes=[
                pltpu.VMEM((rows, width), bf16),
                *[pltpu.VMEM((width,), f32)] * 4,
                pltpu.VMEM((1, rows), jnp.int32),
                pltpu.VMEM((DEPTH, 2, CHUNK, width), bf16),
                pltpu.VMEM((4, rem_pad, width), bf16),
                pltpu.VMEM((rows, width), bf16),
                pltpu.VMEM((rows, width), f32),
                pltpu.VMEM((n_vp, rows, width), f32),
                pltpu.VMEM((2 * n_chunks, rows, CHUNK), f32),
                pltpu.VMEM((2 * n_chunks, rows, CHUNK), f32),
                pltpu.VMEM((2 * n_chunks, rows, CHUNK), f32),
                pltpu.VMEM((n_chunks, rows, CHUNK), f32),
                pltpu.VMEM((rows, LANES), f32),
                pltpu.VMEM((rows, LANES), f32),
                pltpu.VMEM((4, 8, LANES), f32),
                pltpu.VMEM((4, 8, LANES), f32),
                pltpu.VMEM((n_vp * 4, 8, LANES), f32),
                dma((6,)), dma((DEPTH, 2)), dma((4,)),
                dma((3,)), dma((3,)), dma((3,)), dma((3,)),
                dma((2 * n_chunks,)), dma((2 * n_chunks,)),
                dma((n_chunks,)), dma((n_chunks,)),
                dma((n_vp - 1,)), dma((n_vp - 1,)),
                dma((n_vp * 4 - 1,)), dma((n_vp * 4 - 1,)),
            ],
            compiler_params=pltpu.CompilerParams(
                collective_id=0, has_side_effects=True, vmem_limit_bytes=52 * 1024 * 1024
            ),
            name="head",
        )(
            *[
                pltpu.with_memory_space_constraint(a, pltpu.HBM)
                for a in (hidden, lnf_gain, lnf_bias, emb_table, next_tok.reshape(1, rows), eln_gain, eln_bias)
            ]
        )
        logprobs, log_sum, next_in = pl.pallas_call(
            functools.partial(finish_kernel, n_full, rem),
            out_shape=(
                jax.ShapeDtypeStruct((rows, seg), f32),
                jax.ShapeDtypeStruct((1, rows), f32),
                jax.ShapeDtypeStruct((rows, width), bf16),
            ),
            in_specs=[vmem, vmem, vmem],
            out_specs=(hbm, vmem, vmem),
            scratch_shapes=[pltpu.VMEM((rows, seg), f32), dma((rows // 8,))],
            compiler_params=pltpu.CompilerParams(vmem_limit_bytes=24 * 1024 * 1024),
            name="finish",
        )(logits, lse, next_rows)
        return logprobs, log_sum.reshape(rows), next_in

    return jax.shard_map(
        per_device,
        mesh=mesh,
        in_specs=(P("dp", "tp"), P("tp"), P("tp"), P("vp", "tp"), P("dp"), P("tp"), P("tp")),
        out_specs=(P("dp", ("vp", "tp")), P("dp"), P("dp", "tp")),
        check_vma=False,
    )
```

time: 394 us -> 111 us (0.28)
  waiting for transfers between devices: 259 us -> 0 us
  Pallas kernels: 0 us -> 110 us
  blocking collectives: 67.1 us -> 0 us
  matrix products: 28 us -> 0 us
  other arithmetic: 15.7 us -> 0 us
  between operations: 14.1 us -> 0.64 us
  local copies, waits for them, and re-layouts: 10.1 us -> 0 us
    unnamed x3 -> x0, waiting for transfers between devices: 222 us -> none
    pallas_call x0 -> x2, Pallas kernels: none -> 110 us  [the longest x1 107 us: per_device(): pl.pallas_call(functools.partial(head_kernel, n_vp, n_full, rem, width),...]
    psum x1 -> x0, waiting for transfers between devices: 37.1 us -> none  [per_device(): tok_rows = lax.psum(picked, 'vp')]
    psum x2 -> x0, blocking collectives: 35.2 us -> none  [the longest x1 29.5 us: global_lse(): lax.psum(jnp.sum(jnp.exp(logits - row_top[:, None]), axis=1), ('vp', 'tp'))]
    pmax x1 -> x0, blocking collectives: 32 us -> none  [global_lse(): row_top = lax.pmax(jnp.max(logits, axis=1), ('vp', 'tp'))]
    unnamed x1 -> x0, matrix products: 28 us -> none
    unnamed x9 -> x0, local copies, waits for them, and re-layouts: 7.47 us -> none
    reduce_sum x3 -> x0, other arithmetic: 4.75 us -> none  [the longest x1 2.83 us: global_lse(): jnp.sum(jnp.exp(logits - row_top[:, None]), axis=1)]
  transfers between devices with their start and end apart: 2 -> 0, of which waited for: 2 -> 0; matrix products, arithmetic and copies ran while one was open for 0% -> 0% of each run, Pallas kernels for 0% -> 0%
where the time goes in v1:
time: 111 us
  Pallas kernels  110 us (99%)
    pallas_call x1, Pallas kernels, per_device(): pl.pallas_call(functools.partial(head_kernel, n_vp, n_full, rem, width),...  107 us
    pallas_call x1, Pallas kernels, per_device(): pl.pallas_call(functools.partial(finish_kernel, n_full, rem), out_shape=(...  2.8 us

profile of v1, /device:TPU:0, one launch (start us, length us, event | category | flops | bytes accessed | tf_op | source)
XLA Modules:
  0.0 110.7 jit_solution(17603164879892953341)
XLA Ops:
  0.6 107.3 %head.1 = (f32[16,64,1024]{2,1,0:T(8,128)S(1)}, f32[8,128]{1,0:T(8,128)S(1)}, bf16[64,384]{1,0:T(8,128)(2,1)S(1)}) custom-call(bf16[64,384]{1,0:T(8,128)(2,1)} %hid_hbm.1, f32[384]{0:T(512)} %gain1_hbm.1, f32[384]{0:T(512)} %bias1_hbm.1, bf16[62720,384]{1,0:T(8,128)(2,1)} %tab_hbm.1, s32[1,64]{1,0:T(1,128)} %bitcast.2, f32[384]{0:T(512)} %gain2_hbm.1, ...), custom_call_target="tpu_custom_call" | custom-call | tf_op jit(solution)/shard_map/head/pallas_call | solution.py:362
  107.9 2.8 %finish.1 = (f32[64,15680]{1,0:T(8,128)}, f32[1,64]{1,0:T(1,128)}, bf16[64,384]{1,0:T(8,128)(2,1)}) custom-call(f32[16,64,1024]{2,1,0:T(8,128)S(1)} %get-tuple-element.9.logits, f32[8,128]{1,0:T(8,128)S(1)} %get-tuple-element.10.lse, bf16[64,384]{1,0:T(8,128)(2,1)S(1)} %get-tuple-element.11.next_rows), custom_call_target="tpu_custom_call" | custom-call | tf_op jit(solution)/shard_map/finish/pallas_call | solution.py:406

commit v2 on v1

--- a/solution.py
+++ b/solution.py
@@ -8,9 +8,10 @@
 from jax.sharding import PartitionSpec as P
 
 NORM_EPS = 1e-5
-CHUNK = 1024
+CHUNK = 768
 LANES = 128
 DEPTH = 3
+LOWEST = -3.0e38
 MESH = pl.DeviceIdType.MESH
 
 
@@ -21,7 +22,7 @@
     hid, gain1, bias1, gain2, bias2, tok, tab, tab_rem, normed, picked, picked_rx,
     tx, rx, acc, y_rx, m_run, s_run, stat_slots, stat2_slots, lse_slots,
     in_sem, tab_sem, rem_sem, stat_send, stat_recv, stat2_send, stat2_recv,
-    tx_send, tx_recv, y_send, y_recv, pick_send, pick_recv, lse_send, lse_recv,
+    tx_send, tx_recv, y_send, y_recv, pick_send, pick_recv, lse_send, lse_recv, near_sem,
 ):
     rows = hid.shape[0]
     n_chunks = n_full + 1
@@ -44,9 +45,28 @@
     def peer_id(dz, dt):
         return {"vp": lax.rem(vp + dz, n_vp), "tp": lax.rem(tp + dt, 4)}
 
+    hid_copy = pltpu.make_async_copy(hid_hbm, hid, in_sem.at[0])
+    hid_copy.start()
+
+    has_low = jnp.where(vp > 0, 1, 0)
+    has_high = jnp.where(vp < n_vp - 1, 1, 0)
+
+    def signal_vp(sem):
+        @pl.when(vp > 0)
+        def _():
+            pl.semaphore_signal(sem, inc=1, device_id={"vp": vp - 1}, device_id_type=MESH)
+
+        @pl.when(vp < n_vp - 1)
+        def _():
+            pl.semaphore_signal(sem, inc=1, device_id={"vp": vp + 1}, device_id_type=MESH)
+
+    def signal_tp(sem):
+        for dt in (2, 3, 1):
+            pl.semaphore_signal(sem, inc=1, device_id=peer_id(0, dt), device_id_type=MESH)
+
     barrier = pltpu.get_barrier_semaphore()
-    for dz, dt, _ in peers:
-        pl.semaphore_signal(barrier, inc=1, device_id=peer_id(dz, dt), device_id_type=MESH)
+    signal_tp(barrier)
+    signal_vp(barrier)
 
     def seg_start(phase, which):
         y = chip_y + (1 - phase) * (1 - 2 * chip_y)
@@ -75,7 +95,6 @@
         )
 
     small = [
-        pltpu.make_async_copy(hid_hbm, hid, in_sem.at[0]),
         pltpu.make_async_copy(gain1_hbm, gain1, in_sem.at[1]),
         pltpu.make_async_copy(bias1_hbm, bias1, in_sem.at[2]),
         pltpu.make_async_copy(gain2_hbm, gain2, in_sem.at[3]),
@@ -84,29 +103,25 @@
     ]
     for copy in small:
         copy.start()
+    for which in range(2):
+        rem_copy(0, which).start()
     for i in range(min(DEPTH - 1, 2 * n_full)):
         for which in range(2):
             tab_copy(i, which).start()
-    for phase in range(2):
-        for which in range(2):
-            rem_copy(phase, which).start()
+    for which in range(2):
+        rem_copy(1, which).start()
 
     picked[...] = jnp.zeros_like(picked)
-    m_run[...] = jnp.full_like(m_run, -jnp.inf)
+    m_run[...] = jnp.full_like(m_run, LOWEST)
     s_run[...] = jnp.zeros_like(s_run)
-    empty = jnp.zeros((1, 8, LANES), jnp.float32)
-    stat_slots[pl.ds(tp, 1)] = empty
-    stat2_slots[pl.ds(tp, 1)] = empty
-    lse_slots[pl.ds(my_rank, 1)] = empty
     tab_rem[:, rem:, :] = jnp.zeros((4, rem_pad - rem, width), jnp.bfloat16)
 
     lane = lax.broadcasted_iota(jnp.int32, (rows, LANES), 1)
 
-    def stat_tile(x):
+    def stat_row(x):
         s1 = jnp.sum(x, axis=1, keepdims=True)
         s2 = jnp.sum(x * x, axis=1, keepdims=True)
-        both = jnp.where(lane == 0, s1, jnp.where(lane == 1, s2, 0.0))
-        return both.T[:8, :]
+        return jnp.broadcast_to(jnp.concatenate([s1, s2], axis=0), (LANES, LANES)).T[0:1, :]
 
     def stat_copy(slots, send, recv, d):
         return pltpu.make_async_remote_copy(
@@ -115,12 +130,13 @@
         )
 
     def norm(x, slots, send, recv, gain, bias):
-        for d in (2, 3, 1):
+        for d in (1, 2, 3):
             stat_copy(slots, send, recv, d).wait_recv()
         total = (slots[0] + slots[1]) + (slots[2] + slots[3])
         full_width = 4.0 * width
-        mean = total[0:1, :] / full_width
-        var = total[1:2, :] / full_width - mean * mean
+        total = jnp.broadcast_to(total, (8, LANES)) / full_width
+        mean = total
+        var = pltpu.roll(total, rows, axis=1) - mean * mean
         inv = lax.rsqrt(var + NORM_EPS)
         row = lax.broadcasted_iota(jnp.int32, (8, LANES), 0)
         back = jnp.where(row == 0, mean, inv).T
@@ -128,12 +144,12 @@
         inv_c = back[:rows, 1:2]
         return (x - mean_c) * inv_c * gain + bias
 
-    small[0].wait()
+    hid_copy.wait()
     x1 = hid[...].astype(jnp.float32)
-    stat_slots[pl.ds(tp, 1), :, 0:rows] = stat_tile(x1)[None]
-    for copy in small[1:]:
+    stat_slots[pl.ds(tp, 1)] = stat_row(x1)[None]
+    for copy in small:
         copy.wait()
-    pl.semaphore_wait(barrier, len(peers))
+    pl.semaphore_wait(barrier, 3 + has_low + has_high)
     for d in (2, 3, 1):
         stat_copy(stat_slots, stat_send, stat_recv, d).start()
     normed[...] = norm(
@@ -170,8 +186,29 @@
             hot, block, (((1,), (0,)), ((), ())), preferred_element_type=jnp.float32
         )
 
+    def add_picked_rem(phase, which):
+        at = lax.broadcasted_iota(jnp.int32, (rows, rem_pad), 1)
+        hit = (at == tok_local - rem_start(phase, which)) & (at < rem)
+        hot = jnp.where(hit, 1.0, 0.0).astype(jnp.bfloat16)
+        picked[...] += lax.dot_general(
+            hot, tab_rem[phase * 2 + which], (((1,), (0,)), ((), ())), preferred_element_type=jnp.float32
+        )
+
     def run_phase(phase):
         base = phase * n_chunks
+
+        last = base + n_full
+        rem_copy(phase, 0).wait()
+        tx[last, :, 0:rem_pad] = partial(tab_rem[phase * 2])
+        rem_copy(phase, 1).wait()
+        acc[last, :, 0:rem_pad] = partial(tab_rem[phase * 2 + 1])
+        tx_copy(last, rem_pad).start()
+        add_picked_rem(phase, 0)
+        add_picked_rem(phase, 1)
+        tx_copy(last, rem_pad).wait_recv()
+        acc[last, :, 0:rem_pad] = acc[last, :, 0:rem_pad] + rx[last, :, 0:rem_pad]
+        if phase == 0:
+            y_copy(n_full, rem_pad).start()
 
         def body(i, carry):
             k = i - phase * n_full
@@ -193,40 +230,27 @@
             def _():
                 tx_copy(e - 1).wait_recv()
                 acc[e - 1] = acc[e - 1] + rx[e - 1]
+                if phase == 0:
+                    y_copy(e - 1).start()
 
             add_picked(tab[slot, 0], row_start(i, 0))
             add_picked(tab[slot, 1], row_start(i, 1))
-            if phase == 0:
-                @pl.when(k > 0)
-                def _():
-                    y_copy(e - 1).start()
             return carry
 
         lax.fori_loop(phase * n_full, (phase + 1) * n_full, body, 0)
-        last = base + n_full
-        rem_copy(phase, 0).wait()
-        tx[last, :, 0:rem_pad] = partial(tab_rem[phase * 2])
-        rem_copy(phase, 1).wait()
-        acc[last, :, 0:rem_pad] = partial(tab_rem[phase * 2 + 1])
-        tx_copy(last, rem_pad).start()
-        tx_copy(last - 1).wait_recv()
-        acc[last - 1] = acc[last - 1] + rx[last - 1]
-        for which in range(2):
-            block = tab_rem[phase * 2 + which]
-            at = lax.broadcasted_iota(jnp.int32, (rows, rem_pad), 1)
-            hit = (at == tok_local - rem_start(phase, which)) & (at < rem)
-            hot = jnp.where(hit, 1.0, 0.0).astype(jnp.bfloat16)
-            picked[...] += lax.dot_general(
-                hot, block, (((1,), (0,)), ((), ())), preferred_element_type=jnp.float32
-            )
+        end = last - 1
+        tx_copy(end).wait_recv()
+        acc[end] = acc[end] + rx[end]
         if phase == 0:
-            y_copy(last - 1).start()
-        tx_copy(last, rem_pad).wait_recv()
-        acc[last, :, 0:rem_pad] = acc[last, :, 0:rem_pad] + rx[last, :, 0:rem_pad]
-
+            y_copy(end).start()
+
+    signal_vp(near_sem.at[0])
     run_phase(0)
-    y_copy(n_full, rem_pad).start()
+    pl.semaphore_wait(near_sem.at[0], has_low + has_high)
+    signal_vp(near_sem.at[1])
     run_phase(1)
+    pl.semaphore_wait(near_sem.at[1], has_low + has_high)
+    signal_tp(near_sem.at[2])
 
     def pick_copy(dz):
         return pltpu.make_async_remote_copy(
@@ -242,7 +266,7 @@
     x2 = picked_rx[0]
     for z in range(1, n_vp):
         x2 = x2 + picked_rx[z]
-    stat2_slots[pl.ds(tp, 1), :, 0:rows] = stat_tile(x2)[None]
+    stat2_slots[pl.ds(tp, 1)] = stat_row(x2)[None]
     for d in (2, 3, 1):
         stat_copy(stat2_slots, stat2_send, stat2_recv, d).start()
     next_out[...] = norm(
@@ -274,15 +298,16 @@
         absorb(k, CHUNK)
         return carry
 
-    lax.fori_loop(0, n_full, absorb_body, 0)
     y_copy(n_full, rem_pad).wait_recv()
     absorb(n_full, rem_pad)
+    pl.semaphore_wait(near_sem.at[2], 3)
+    lax.fori_loop(0, n_full, absorb_body, 0)
 
     m_t = m_run[...].T
     top = jnp.max(m_t, axis=0, keepdims=True)
     tot = jnp.sum(s_run[...].T * jnp.exp(m_t - top), axis=0, keepdims=True)
-    row = lax.broadcasted_iota(jnp.int32, (8, rows), 0)
-    lse_slots[pl.ds(my_rank, 1), :, 0:rows] = jnp.where(row == 0, top, tot)[None]
+    lse_slots[pl.ds(my_rank, 1), :, 0:rows] = top[None]
+    lse_slots[pl.ds(my_rank, 1), :, rows:LANES] = tot[None]
 
     def lse_copy(dz, dt, j):
         return pltpu.make_async_remote_copy(
@@ -312,18 +337,22 @@
 
     for dz, dt, j in peers:
         lse_copy(dz, dt, j).wait_recv()
-    tops = [lse_slots[r, 0:1, :] for r in range(n_vp * 4)]
-    top = functools.reduce(jnp.maximum, tops)
-    tot = functools.reduce(
-        jnp.add, [lse_slots[r, 1:2, :] * jnp.exp(tops[r] - top) for r in range(n_vp * 4)]
-    )
+    pairs = lse_slots[:, 0, :]
+    top = jnp.max(pairs, axis=0, keepdims=True)
+    scaled = pltpu.roll(pairs, rows, axis=1) * jnp.exp(pairs - top)
+    tot = jnp.sum(scaled, axis=0, keepdims=True)
     lse_out[...] = jnp.broadcast_to(top + jnp.log(tot), (8, LANES))
     for dz, dt, j in peers:
         lse_copy(dz, dt, j).wait_send()
 
 
-def finish_kernel(n_full, rem, logits, lse, next_rows, out_hbm, sum_out, next_out, stage, sem):
+def finish_kernel(n_full, rem, logits, lse, next_rows, out_hbm, sum_hbm, next_hbm, stage, sums, sem, small_sem):
     rows = stage.shape[0]
+    next_copy = pltpu.make_async_copy(next_rows, next_hbm, small_sem.at[0])
+    next_copy.start()
+    sums[...] = lse[0:1, 0:rows]
+    sum_copy = pltpu.make_async_copy(sums, sum_hbm, small_sem.at[1])
+    sum_copy.start()
     log_sum = lse[...].T[:rows, 0:1]
     copies = []
     for r in range(rows // 8):
@@ -338,9 +367,7 @@
         copy = pltpu.make_async_copy(stage.at[here, :], out_hbm.at[here, :], sem.at[r])
         copy.start()
         copies.append(copy)
-    sum_out[...] = lse[0:1, 0:rows]
-    next_out[...] = next_rows[...]
-    for copy in copies:
+    for copy in [next_copy, sum_copy] + copies:
         copy.wait()
 
 
@@ -354,11 +381,11 @@
         n_full, rem = divmod(seg, CHUNK)
         n_chunks = n_full + 1
         rem_pad = -(-rem // LANES) * LANES
+        assert 2 * rows == LANES and n_vp == 4 and rem
         f32, bf16 = jnp.float32, jnp.bfloat16
         dma = pltpu.SemaphoreType.DMA
         hbm = pl.BlockSpec(memory_space=pltpu.HBM)
         vmem = pl.BlockSpec(memory_space=pltpu.VMEM)
-        big = (64 * 1024 * 1024)
         logits, lse, next_rows = pl.pallas_call(
             functools.partial(head_kernel, n_vp, n_full, rem, width),
             out_shape=(
@@ -383,15 +410,16 @@
                 pltpu.VMEM((n_chunks, rows, CHUNK), f32),
                 pltpu.VMEM((rows, LANES), f32),
                 pltpu.VMEM((rows, LANES), f32),
-                pltpu.VMEM((4, 8, LANES), f32),
-                pltpu.VMEM((4, 8, LANES), f32),
-                pltpu.VMEM((n_vp * 4, 8, LANES), f32),
+                pltpu.VMEM((4, 1, LANES), f32),
+                pltpu.VMEM((4, 1, LANES), f32),
+                pltpu.VMEM((n_vp * 4, 1, LANES), f32),
                 dma((6,)), dma((DEPTH, 2)), dma((4,)),
                 dma((3,)), dma((3,)), dma((3,)), dma((3,)),
                 dma((2 * n_chunks,)), dma((2 * n_chunks,)),
                 dma((n_chunks,)), dma((n_chunks,)),
                 dma((n_vp - 1,)), dma((n_vp - 1,)),
                 dma((n_vp * 4 - 1,)), dma((n_vp * 4 - 1,)),
+                pltpu.SemaphoreType.REGULAR((3,)),
             ],
             compiler_params=pltpu.CompilerParams(
                 collective_id=0, has_side_effects=True, vmem_limit_bytes=52 * 1024 * 1024
@@ -411,8 +439,8 @@
                 jax.ShapeDtypeStruct((rows, width), bf16),
             ),
             in_specs=[vmem, vmem, vmem],
-            out_specs=(hbm, vmem, vmem),
-            scratch_shapes=[pltpu.VMEM((rows, seg), f32), dma((rows // 8,))],
+            out_specs=(hbm, hbm, hbm),
+            scratch_shapes=[pltpu.VMEM((rows, seg), f32), pltpu.VMEM((1, rows), f32), dma((rows // 8,)), dma((2,))],
             compiler_params=pltpu.CompilerParams(vmem_limit_bytes=24 * 1024 * 1024),
             name="finish",
         )(logits, lse, next_rows)

time: 111 us -> 109 us (0.982)
  Pallas kernels: 110 us -> 108 us
    pallas_call x1, Pallas kernels: 107 us -> 106 us  [per_device(): pl.pallas_call(functools.partial(head_kernel, n_vp, n_full, rem, width),...]
where the time goes in v2:
time: 109 us
  Pallas kernels  108 us (99%)
    pallas_call x1, Pallas kernels, per_device(): pl.pallas_call(functools.partial(head_kernel, n_vp, n_full, rem, width),...  106 us
    pallas_call x1, Pallas kernels, per_device(): pl.pallas_call(functools.partial(finish_kernel, n_full, rem), out_shape=(...  2.2 us

profile of v2, /device:TPU:0, one launch (start us, length us, event | category | flops | bytes accessed | tf_op | source)
XLA Modules:
  0.0 108.9 jit_solution(527645095156823388)
XLA Ops:
  0.6 106.1 %head.1 = (f32[21,64,768]{2,1,0:T(8,128)S(1)}, f32[8,128]{1,0:T(8,128)S(1)}, bf16[64,384]{1,0:T(8,128)(2,1)S(1)}) custom-call(bf16[64,384]{1,0:T(8,128)(2,1)} %hid_hbm.1, f32[384]{0:T(512)} %gain1_hbm.1, f32[384]{0:T(512)} %bias1_hbm.1, bf16[62720,384]{1,0:T(8,128)(2,1)} %tab_hbm.1, s32[1,64]{1,0:T(1,128)} %bitcast.2, f32[384]{0:T(512)} %gain2_hbm.1, ...), custom_call_target="tpu_custom_call" | custom-call | tf_op jit(solution)/shard_map/head/pallas_call | solution.py:389
  106.7 2.2 %finish.1 = (f32[64,15680]{1,0:T(8,128)}, f32[1,64]{1,0:T(1,128)}, bf16[64,384]{1,0:T(8,128)(2,1)}) custom-call(f32[21,64,768]{2,1,0:T(8,128)S(1)} %get-tuple-element.9.logits, f32[8,128]{1,0:T(8,128)S(1)} %get-tuple-element.10.lse, bf16[64,384]{1,0:T(8,128)(2,1)S(1)} %get-tuple-element.11.next_rows), custom_call_target="tpu_custom_call" | custom-call | tf_op jit(solution)/shard_map/finish/pallas_call | solution.py:434

commit v3 on v2

--- a/solution.py
+++ b/solution.py
@@ -22,7 +22,7 @@
     hid, gain1, bias1, gain2, bias2, tok, tab, tab_rem, normed, picked, picked_rx,
     tx, rx, acc, y_rx, m_run, s_run, stat_slots, stat2_slots, lse_slots,
     in_sem, tab_sem, rem_sem, stat_send, stat_recv, stat2_send, stat2_recv,
-    tx_send, tx_recv, y_send, y_recv, pick_send, pick_recv, lse_send, lse_recv, near_sem,
+    tx_send, tx_recv, y_send, y_recv, pick_send, pick_recv, lse_send, lse_recv, near_sem, y_tail, y_tail_rx,
 ):
     rows = hid.shape[0]
     n_chunks = n_full + 1
@@ -101,15 +101,6 @@
         pltpu.make_async_copy(bias2_hbm, bias2, in_sem.at[4]),
         pltpu.make_async_copy(tok_hbm, tok, in_sem.at[5]),
     ]
-    for copy in small:
-        copy.start()
-    for which in range(2):
-        rem_copy(0, which).start()
-    for i in range(min(DEPTH - 1, 2 * n_full)):
-        for which in range(2):
-            tab_copy(i, which).start()
-    for which in range(2):
-        rem_copy(1, which).start()
 
     picked[...] = jnp.zeros_like(picked)
     m_run[...] = jnp.full_like(m_run, LOWEST)
@@ -147,11 +138,20 @@
     hid_copy.wait()
     x1 = hid[...].astype(jnp.float32)
     stat_slots[pl.ds(tp, 1)] = stat_row(x1)[None]
-    for copy in small:
-        copy.wait()
     pl.semaphore_wait(barrier, 3 + has_low + has_high)
     for d in (2, 3, 1):
         stat_copy(stat_slots, stat_send, stat_recv, d).start()
+    for copy in small:
+        copy.start()
+    for which in range(2):
+        rem_copy(0, which).start()
+    for i in range(min(DEPTH - 1, 2 * n_full)):
+        for which in range(2):
+            tab_copy(i, which).start()
+    for which in range(2):
+        rem_copy(1, which).start()
+    for copy in small:
+        copy.wait()
     normed[...] = norm(
         x1, stat_slots, stat_send, stat_recv, gain1[...].reshape(1, width), bias1[...].reshape(1, width)
     ).astype(jnp.bfloat16)
@@ -163,12 +163,36 @@
             device_id={"tp": sibling}, device_id_type=MESH,
         )
 
-    def y_copy(e, cols=None):
-        view = (lambda r: r.at[e]) if cols is None else (lambda r: r.at[e, :, pl.ds(0, cols)])
-        return pltpu.make_async_remote_copy(
-            src_ref=view(acc), dst_ref=view(y_rx), send_sem=y_send.at[e], recv_sem=y_recv.at[e],
+    def y_copy(e):
+        return pltpu.make_async_remote_copy(
+            src_ref=acc.at[e], dst_ref=y_rx.at[e], send_sem=y_send.at[e], recv_sem=y_recv.at[e],
             device_id={"tp": across}, device_id_type=MESH,
         )
+
+    half = LANES // 2
+    whole = rem - half
+
+    def y_tail_copy():
+        return pltpu.make_async_remote_copy(
+            src_ref=y_tail, dst_ref=y_tail_rx, send_sem=y_send.at[n_full], recv_sem=y_recv.at[n_full],
+            device_id={"tp": across}, device_id_type=MESH,
+        )
+
+    def pack_tail(block):
+        y_tail[0:rows, :] = block[:, 0:whole]
+        low = block[0:rows // 2, whole:whole + LANES]
+        high = pltpu.roll(block[rows // 2:rows, whole:whole + LANES], half, axis=1)
+        both = jnp.where(lane[0:rows // 2] < half, low, high)
+        y_tail[rows:rows + rows // 4, 0:LANES] = both[0:rows // 4]
+        y_tail[rows:rows + rows // 4, LANES:2 * LANES] = both[rows // 4:rows // 2]
+
+    def tail_block(b):
+        if (b + 1) * LANES <= whole:
+            return y_tail_rx[0:rows, b * LANES:(b + 1) * LANES]
+        both = jnp.concatenate(
+            [y_tail_rx[rows:rows + rows // 4, 0:LANES], y_tail_rx[rows:rows + rows // 4, LANES:2 * LANES]], axis=0
+        )
+        return jnp.concatenate([both, pltpu.roll(both, half, axis=1)], axis=0)
 
     def partial(block):
         return lax.dot_general(
@@ -198,17 +222,39 @@
         base = phase * n_chunks
 
         last = base + n_full
+        first = phase * n_full
+        slot0 = first % DEPTH
         rem_copy(phase, 0).wait()
         tx[last, :, 0:rem_pad] = partial(tab_rem[phase * 2])
+        tx_copy(last, rem_pad).start()
+        tab_copy(first, 0).wait()
+        tx[base] = partial(tab[slot0, 0])
+        tx_copy(base).start()
         rem_copy(phase, 1).wait()
-        acc[last, :, 0:rem_pad] = partial(tab_rem[phase * 2 + 1])
-        tx_copy(last, rem_pad).start()
+        mine = partial(tab_rem[phase * 2 + 1])
+        acc[last, :, 0:rem_pad] = mine
+        tab_copy(first, 1).wait()
+        acc[base] = partial(tab[slot0, 1])
+        tx_copy(last, rem_pad).wait_recv()
+        if phase == 0:
+            pack_tail(acc[last, :, 0:rem_pad] + rx[last, :, 0:rem_pad])
+            y_tail_copy().start()
+        else:
+            acc[last, :, 0:rem_pad] = acc[last, :, 0:rem_pad] + rx[last, :, 0:rem_pad]
+
+        def finish(e):
+            tx_copy(e).wait_recv()
+            acc[e] = acc[e] + rx[e]
+            if phase == 0:
+                y_copy(e).start()
+
+        tab_copy(first + DEPTH - 1, 0).start()
+        tab_copy(first + DEPTH - 1, 1).start()
         add_picked_rem(phase, 0)
         add_picked_rem(phase, 1)
-        tx_copy(last, rem_pad).wait_recv()
-        acc[last, :, 0:rem_pad] = acc[last, :, 0:rem_pad] + rx[last, :, 0:rem_pad]
-        if phase == 0:
-            y_copy(n_full, rem_pad).start()
+        finish(base)
+        add_picked(tab[slot0, 0], row_start(first, 0))
+        add_picked(tab[slot0, 1], row_start(first, 1))
 
         def body(i, carry):
             k = i - phase * n_full
@@ -222,27 +268,20 @@
             slot = lax.rem(i, DEPTH)
             tab_copy(i, 0).wait()
             tx[e] = partial(tab[slot, 0])
+            tx_copy(e).start()
             tab_copy(i, 1).wait()
             acc[e] = partial(tab[slot, 1])
-            tx_copy(e).start()
-
-            @pl.when(k > 0)
+
+            @pl.when(k > 1)
             def _():
-                tx_copy(e - 1).wait_recv()
-                acc[e - 1] = acc[e - 1] + rx[e - 1]
-                if phase == 0:
-                    y_copy(e - 1).start()
+                finish(e - 1)
 
             add_picked(tab[slot, 0], row_start(i, 0))
             add_picked(tab[slot, 1], row_start(i, 1))
             return carry
 
-        lax.fori_loop(phase * n_full, (phase + 1) * n_full, body, 0)
-        end = last - 1
-        tx_copy(end).wait_recv()
-        acc[end] = acc[end] + rx[end]
-        if phase == 0:
-            y_copy(end).start()
+        lax.fori_loop(first + 1, first + n_full, body, 0)
+        finish(last - 1)
 
     signal_vp(near_sem.at[0])
     run_phase(0)
@@ -279,7 +318,7 @@
         top = m_run[...]
         for b in range(blocks):
             sl = pl.ds(b * LANES, LANES)
-            z = acc[e, :, sl] + y_rx[k, :, sl]
+            z = acc[e, :, sl] + (y_rx[k, :, sl] if cols == CHUNK else tail_block(b))
             logits[k, :, sl] = z
             if cols != CHUNK and (b + 1) * LANES > rem:
                 z = jnp.where(lane < rem - b * LANES, z, -jnp.inf)
@@ -298,7 +337,7 @@
         absorb(k, CHUNK)
         return carry
 
-    y_copy(n_full, rem_pad).wait_recv()
+    y_tail_copy().wait_recv()
     absorb(n_full, rem_pad)
     pl.semaphore_wait(near_sem.at[2], 3)
     lax.fori_loop(0, n_full, absorb_body, 0)
@@ -328,7 +367,7 @@
     lax.fori_loop(0, n_full, drain, 0)
     tx_copy(n_full, rem_pad).wait_send()
     tx_copy(n_chunks + n_full, rem_pad).wait_send()
-    y_copy(n_full, rem_pad).wait_send()
+    y_tail_copy().wait_send()
     for d in (1, 2, 3):
         stat_copy(stat_slots, stat_send, stat_recv, d).wait_send()
         stat_copy(stat2_slots, stat2_send, stat2_recv, d).wait_send()
@@ -381,7 +420,7 @@
         n_full, rem = divmod(seg, CHUNK)
         n_chunks = n_full + 1
         rem_pad = -(-rem // LANES) * LANES
-        assert 2 * rows == LANES and n_vp == 4 and rem
+        assert 2 * rows == LANES and n_vp == 4 and rem == 2 * LANES + LANES // 2 and n_full > DEPTH
         f32, bf16 = jnp.float32, jnp.bfloat16
         dma = pltpu.SemaphoreType.DMA
         hbm = pl.BlockSpec(memory_space=pltpu.HBM)
@@ -420,6 +459,7 @@
                 dma((n_vp - 1,)), dma((n_vp - 1,)),
                 dma((n_vp * 4 - 1,)), dma((n_vp * 4 - 1,)),
                 pltpu.SemaphoreType.REGULAR((3,)),
+                pltpu.VMEM((rows + rows // 4, 2 * LANES), f32), pltpu.VMEM((rows + rows // 4, 2 * LANES), f32),
             ],
             compiler_params=pltpu.CompilerParams(
                 collective_id=0, has_side_effects=True, vmem_limit_bytes=52 * 1024 * 1024

time: 109 us -> 108 us (level)
    pallas_call x1, Pallas kernels: 106 us -> 105 us  [per_device(): pl.pallas_call(functools.partial(head_kernel, n_vp, n_full, rem, width),...]
where the time goes in v3:
time: 108 us
  Pallas kernels  107 us (99%)
    pallas_call x1, Pallas kernels, per_device(): pl.pallas_call(functools.partial(head_kernel, n_vp, n_full, rem, width),...  105 us
    pallas_call x1, Pallas kernels, per_device(): pl.pallas_call(functools.partial(finish_kernel, n_full, rem), out_shape=(...  2.2 us

profile of v3, /device:TPU:0, one launch (start us, length us, event | category | flops | bytes accessed | tf_op | source)
XLA Modules:
  0.0 107.8 jit_solution(4847671702000254828)
XLA Ops:
  0.6 104.9 %head.1 = (f32[21,64,768]{2,1,0:T(8,128)S(1)}, f32[8,128]{1,0:T(8,128)S(1)}, bf16[64,384]{1,0:T(8,128)(2,1)S(1)}) custom-call(bf16[64,384]{1,0:T(8,128)(2,1)} %hid_hbm.1, f32[384]{0:T(512)} %gain1_hbm.1, f32[384]{0:T(512)} %bias1_hbm.1, bf16[62720,384]{1,0:T(8,128)(2,1)} %tab_hbm.1, s32[1,64]{1,0:T(1,128)} %bitcast.2, f32[384]{0:T(512)} %gain2_hbm.1, ...), custom_call_target="tpu_custom_call" | custom-call | tf_op jit(solution)/shard_map/head/pallas_call | solution.py:428
  105.6 2.2 %finish.1 = (f32[64,15680]{1,0:T(8,128)}, f32[1,64]{1,0:T(1,128)}, bf16[64,384]{1,0:T(8,128)(2,1)}) custom-call(f32[21,64,768]{2,1,0:T(8,128)S(1)} %get-tuple-element.9.logits, f32[8,128]{1,0:T(8,128)S(1)} %get-tuple-element.10.lse, bf16[64,384]{1,0:T(8,128)(2,1)S(1)} %get-tuple-element.11.next_rows), custom_call_target="tpu_custom_call" | custom-call | tf_op jit(solution)/shard_map/finish/pallas_call | solution.py:474

commit v4 on v3

--- a/solution.py
+++ b/solution.py
@@ -8,7 +8,7 @@
 from jax.sharding import PartitionSpec as P
 
 NORM_EPS = 1e-5
-CHUNK = 768
+CHUNK = 512
 LANES = 128
 DEPTH = 3
 LOWEST = -3.0e38

time: 108 us -> 109 us (level)
  no operation moved by 1% of the time
where the time goes in v4:
time: 109 us
  Pallas kernels  108 us (99%)
    pallas_call x1, Pallas kernels, per_device(): pl.pallas_call(functools.partial(head_kernel, n_vp, n_full, rem, width),...  106 us
    pallas_call x1, Pallas kernels, per_device(): pl.pallas_call(functools.partial(finish_kernel, n_full, rem), out_shape=(...  2.2 us

profile of v4, /device:TPU:0, one launch (start us, length us, event | category | flops | bytes accessed | tf_op | source)
XLA Modules:
  0.0 108.5 jit_solution(11098353026332093243)
XLA Ops:
  0.6 105.7 %head.1 = (f32[31,64,512]{2,1,0:T(8,128)S(1)}, f32[8,128]{1,0:T(8,128)S(1)}, bf16[64,384]{1,0:T(8,128)(2,1)S(1)}) custom-call(bf16[64,384]{1,0:T(8,128)(2,1)} %hid_hbm.1, f32[384]{0:T(512)} %gain1_hbm.1, f32[384]{0:T(512)} %bias1_hbm.1, bf16[62720,384]{1,0:T(8,128)(2,1)} %tab_hbm.1, s32[1,64]{1,0:T(1,128)} %bitcast.2, f32[384]{0:T(512)} %gain2_hbm.1, ...), custom_call_target="tpu_custom_call" | custom-call | tf_op jit(solution)/shard_map/head/pallas_call | solution.py:428
  106.3 2.2 %finish.1 = (f32[64,15680]{1,0:T(8,128)}, f32[1,64]{1,0:T(1,128)}, bf16[64,384]{1,0:T(8,128)(2,1)}) custom-call(f32[31,64,512]{2,1,0:T(8,128)S(1)} %get-tuple-element.9.logits, f32[8,128]{1,0:T(8,128)S(1)} %get-tuple-element.10.lse, bf16[64,384]{1,0:T(8,128)(2,1)S(1)} %get-tuple-element.11.next_rows), custom_call_target="tpu_custom_call" | custom-call | tf_op jit(solution)/shard_map/finish/pallas_call | solution.py:474

commit v5 on v3

--- a/solution.py
+++ b/solution.py
@@ -169,6 +169,22 @@
             device_id={"tp": across}, device_id_type=MESH,
         )
 
+    def y_pair(e):
+        return pltpu.make_async_remote_copy(
+            src_ref=acc.at[pl.ds(e, 2)], dst_ref=y_rx.at[pl.ds(e, 2)],
+            send_sem=y_send.at[e + 1], recv_sem=y_recv.at[e + 1],
+            device_id={"tp": across}, device_id_type=MESH,
+        )
+
+    def opens_pair(k):
+        return (lax.rem(k + core, 2) == 0) & (k < n_full - 1)
+
+    def closes_pair(k):
+        return (lax.rem(k + core, 2) == 1) & (k > 0)
+
+    def is_single(k):
+        return (core == 1) & ((k == 0) | (k == n_full - 1))
+
     half = LANES // 2
     whole = rem - half
 
@@ -246,7 +262,13 @@
             tx_copy(e).wait_recv()
             acc[e] = acc[e] + rx[e]
             if phase == 0:
-                y_copy(e).start()
+                @pl.when(closes_pair(e))
+                def _():
+                    y_pair(e - 1).start()
+
+                @pl.when(is_single(e))
+                def _():
+                    y_copy(e).start()
 
         tab_copy(first + DEPTH - 1, 0).start()
         tab_copy(first + DEPTH - 1, 1).start()
@@ -333,7 +355,14 @@
         s_run[...] = total
 
     def absorb_body(k, carry):
-        y_copy(k).wait_recv()
+        @pl.when(opens_pair(k))
+        def _():
+            y_pair(k).wait_recv()
+
+        @pl.when(is_single(k))
+        def _():
+            y_copy(k).wait_recv()
+
         absorb(k, CHUNK)
         return carry
 
@@ -361,7 +390,15 @@
     def drain(e, carry):
         tx_copy(e).wait_send()
         tx_copy(n_chunks + e).wait_send()
-        y_copy(e).wait_send()
+
+        @pl.when(opens_pair(e))
+        def _():
+            y_pair(e).wait_send()
+
+        @pl.when(is_single(e))
+        def _():
+            y_copy(e).wait_send()
+
         return carry
 
     lax.fori_loop(0, n_full, drain, 0)
@@ -420,7 +457,7 @@
         n_full, rem = divmod(seg, CHUNK)
         n_chunks = n_full + 1
         rem_pad = -(-rem // LANES) * LANES
-        assert 2 * rows == LANES and n_vp == 4 and rem == 2 * LANES + LANES // 2 and n_full > DEPTH
+        assert 2 * rows == LANES and n_vp == 4 and rem == 2 * LANES + LANES // 2 and n_full > DEPTH and n_full % 2 == 0
         f32, bf16 = jnp.float32, jnp.bfloat16
         dma = pltpu.SemaphoreType.DMA
         hbm = pl.BlockSpec(memory_space=pltpu.HBM)

time: 108 us -> 108 us (level)
  no operation moved by 1% of the time
where the time goes in v5:
time: 108 us
  Pallas kernels  107 us (99%)
    pallas_call x1, Pallas kernels, per_device(): pl.pallas_call(functools.partial(head_kernel, n_vp, n_full, rem, width),...  105 us
    pallas_call x1, Pallas kernels, per_device(): pl.pallas_call(functools.partial(finish_kernel, n_full, rem), out_shape=(...  2.2 us

profile of v5, /device:TPU:0, one launch (start us, length us, event | category | flops | bytes accessed | tf_op | source)
XLA Modules:
  0.0 107.9 jit_solution(5247468952250321490)
XLA Ops:
  0.6 105.1 %head.1 = (f32[21,64,768]{2,1,0:T(8,128)S(1)}, f32[8,128]{1,0:T(8,128)S(1)}, bf16[64,384]{1,0:T(8,128)(2,1)S(1)}) custom-call(bf16[64,384]{1,0:T(8,128)(2,1)} %hid_hbm.1, f32[384]{0:T(512)} %gain1_hbm.1, f32[384]{0:T(512)} %bias1_hbm.1, bf16[62720,384]{1,0:T(8,128)(2,1)} %tab_hbm.1, s32[1,64]{1,0:T(1,128)} %bitcast.2, f32[384]{0:T(512)} %gain2_hbm.1, ...), custom_call_target="tpu_custom_call" | custom-call | tf_op jit(solution)/shard_map/head/pallas_call | solution.py:465
  105.7 2.2 %finish.1 = (f32[64,15680]{1,0:T(8,128)}, f32[1,64]{1,0:T(1,128)}, bf16[64,384]{1,0:T(8,128)(2,1)}) custom-call(f32[21,64,768]{2,1,0:T(8,128)S(1)} %get-tuple-element.9.logits, f32[8,128]{1,0:T(8,128)S(1)} %get-tuple-element.10.lse, bf16[64,384]{1,0:T(8,128)(2,1)S(1)} %get-tuple-element.11.next_rows), custom_call_target="tpu_custom_call" | custom-call | tf_op jit(solution)/shard_map/finish/pallas_call | solution.py:511

commit v6 on v3

--- a/solution.py
+++ b/solution.py
@@ -116,13 +116,15 @@
 
     def stat_copy(slots, send, recv, d):
         return pltpu.make_async_remote_copy(
-            src_ref=slots.at[tp], dst_ref=slots.at[tp], send_sem=send.at[d - 1], recv_sem=recv.at[d - 1],
+            src_ref=slots.at[tp], dst_ref=slots.at[tp], send_sem=send.at[0], recv_sem=recv.at[0],
             device_id=peer_id(0, d), device_id_type=MESH,
         )
 
+    def all_of(slots, sem, count):
+        return pltpu.make_async_copy(slots.at[pl.ds(0, count)], slots.at[pl.ds(0, count)], sem.at[0])
+
     def norm(x, slots, send, recv, gain, bias):
-        for d in (1, 2, 3):
-            stat_copy(slots, send, recv, d).wait_recv()
+        all_of(slots, recv, 3).wait()
         total = (slots[0] + slots[1]) + (slots[2] + slots[3])
         full_width = 4.0 * width
         total = jnp.broadcast_to(total, (8, LANES)) / full_width
@@ -335,11 +337,25 @@
     def absorb_body(k, carry):
         y_copy(k).wait_recv()
         absorb(k, CHUNK)
+        tx_copy(k).wait_send()
+        tx_copy(n_chunks + k).wait_send()
+
+        @pl.when(k > 0)
+        def _():
+            y_copy(k - 1).wait_send()
+
         return carry
 
     y_tail_copy().wait_recv()
     absorb(n_full, rem_pad)
     pl.semaphore_wait(near_sem.at[2], 3)
+    tx_copy(n_full, rem_pad).wait_send()
+    tx_copy(n_chunks + n_full, rem_pad).wait_send()
+    y_tail_copy().wait_send()
+    all_of(stat_slots, stat_send, 3).wait()
+    all_of(stat2_slots, stat2_send, 3).wait()
+    for dz in range(1, n_vp):
+        pick_copy(dz).wait_send()
     lax.fori_loop(0, n_full, absorb_body, 0)
 
     m_t = m_run[...].T
@@ -351,38 +367,21 @@
     def lse_copy(dz, dt, j):
         return pltpu.make_async_remote_copy(
             src_ref=lse_slots.at[my_rank], dst_ref=lse_slots.at[my_rank],
-            send_sem=lse_send.at[j - 1], recv_sem=lse_recv.at[j - 1],
+            send_sem=lse_send.at[0], recv_sem=lse_recv.at[0],
             device_id=peer_id(dz, dt), device_id_type=MESH,
         )
 
     for dz, dt, j in peers:
         lse_copy(dz, dt, j).start()
 
-    def drain(e, carry):
-        tx_copy(e).wait_send()
-        tx_copy(n_chunks + e).wait_send()
-        y_copy(e).wait_send()
-        return carry
-
-    lax.fori_loop(0, n_full, drain, 0)
-    tx_copy(n_full, rem_pad).wait_send()
-    tx_copy(n_chunks + n_full, rem_pad).wait_send()
-    y_tail_copy().wait_send()
-    for d in (1, 2, 3):
-        stat_copy(stat_slots, stat_send, stat_recv, d).wait_send()
-        stat_copy(stat2_slots, stat2_send, stat2_recv, d).wait_send()
-    for dz in range(1, n_vp):
-        pick_copy(dz).wait_send()
-
-    for dz, dt, j in peers:
-        lse_copy(dz, dt, j).wait_recv()
+    y_copy(n_full - 1).wait_send()
+    all_of(lse_slots, lse_recv, len(peers)).wait()
     pairs = lse_slots[:, 0, :]
     top = jnp.max(pairs, axis=0, keepdims=True)
     scaled = pltpu.roll(pairs, rows, axis=1) * jnp.exp(pairs - top)
     tot = jnp.sum(scaled, axis=0, keepdims=True)
     lse_out[...] = jnp.broadcast_to(top + jnp.log(tot), (8, LANES))
-    for dz, dt, j in peers:
-        lse_copy(dz, dt, j).wait_send()
+    all_of(lse_slots, lse_send, len(peers)).wait()
 
 
 def finish_kernel(n_full, rem, logits, lse, next_rows, out_hbm, sum_hbm, next_hbm, stage, sums, sem, small_sem):
@@ -453,11 +452,11 @@
                 pltpu.VMEM((4, 1, LANES), f32),
                 pltpu.VMEM((n_vp * 4, 1, LANES), f32),
                 dma((6,)), dma((DEPTH, 2)), dma((4,)),
-                dma((3,)), dma((3,)), dma((3,)), dma((3,)),
+                dma((1,)), dma((1,)), dma((1,)), dma((1,)),
                 dma((2 * n_chunks,)), dma((2 * n_chunks,)),
                 dma((n_chunks,)), dma((n_chunks,)),
                 dma((n_vp - 1,)), dma((n_vp - 1,)),
-                dma((n_vp * 4 - 1,)), dma((n_vp * 4 - 1,)),
+                dma((1,)), dma((1,)),
                 pltpu.SemaphoreType.REGULAR((3,)),
                 pltpu.VMEM((rows + rows // 4, 2 * LANES), f32), pltpu.VMEM((rows + rows // 4, 2 * LANES), f32),
             ],

time: 108 us -> 108 us (level)
  no operation moved by 1% of the time
where the time goes in v6:
time: 108 us
  Pallas kernels  107 us (99%)
    pallas_call x1, Pallas kernels, per_device(): pl.pallas_call(functools.partial(head_kernel, n_vp, n_full, rem, width),...  105 us
    pallas_call x1, Pallas kernels, per_device(): pl.pallas_call(functools.partial(finish_kernel, n_full, rem), out_shape=(...  2.2 us

profile of v6, /device:TPU:0, one launch (start us, length us, event | category | flops | bytes accessed | tf_op | source)
XLA Modules:
  0.0 107.6 jit_solution(11368016534230521121)
XLA Ops:
  0.6 104.8 %head.1 = (f32[21,64,768]{2,1,0:T(8,128)S(1)}, f32[8,128]{1,0:T(8,128)S(1)}, bf16[64,384]{1,0:T(8,128)(2,1)S(1)}) custom-call(bf16[64,384]{1,0:T(8,128)(2,1)} %hid_hbm.1, f32[384]{0:T(512)} %gain1_hbm.1, f32[384]{0:T(512)} %bias1_hbm.1, bf16[62720,384]{1,0:T(8,128)(2,1)} %tab_hbm.1, s32[1,64]{1,0:T(1,128)} %bitcast.2, f32[384]{0:T(512)} %gain2_hbm.1, ...), custom_call_target="tpu_custom_call" | custom-call | tf_op jit(solution)/shard_map/head/pallas_call | solution.py:427
  105.4 2.2 %finish.1 = (f32[64,15680]{1,0:T(8,128)}, f32[1,64]{1,0:T(1,128)}, bf16[64,384]{1,0:T(8,128)(2,1)}) custom-call(f32[21,64,768]{2,1,0:T(8,128)S(1)} %get-tuple-element.9.logits, f32[8,128]{1,0:T(8,128)S(1)} %get-tuple-element.10.lse, bf16[64,384]{1,0:T(8,128)(2,1)S(1)} %get-tuple-element.11.next_rows), custom_call_target="tpu_custom_call" | custom-call | tf_op jit(solution)/shard_map/finish/pallas_call | solution.py:473

commit v7 on v6

--- a/solution.py
+++ b/solution.py
@@ -165,9 +165,14 @@
             device_id={"tp": sibling}, device_id_type=MESH,
         )
 
-    def y_copy(e):
-        return pltpu.make_async_remote_copy(
-            src_ref=acc.at[e], dst_ref=y_rx.at[e], send_sem=y_send.at[e], recv_sem=y_recv.at[e],
+    middle = n_full - 8
+    sizes = [1, 1, 2] + [4] * (middle // 4) + [middle % 4] * (middle % 4 > 0) + [2, 1, 1]
+    groups = [(sum(sizes[:g]), n) for g, n in enumerate(sizes)]
+
+    def y_copy(e, n):
+        return pltpu.make_async_remote_copy(
+            src_ref=acc.at[pl.ds(e, n)], dst_ref=y_rx.at[pl.ds(e, n)],
+            send_sem=y_send.at[e], recv_sem=y_recv.at[e],
             device_id={"tp": across}, device_id_type=MESH,
         )
 
@@ -248,7 +253,10 @@
             tx_copy(e).wait_recv()
             acc[e] = acc[e] + rx[e]
             if phase == 0:
-                y_copy(e).start()
+                for g, n in groups:
+                    @pl.when(e == g + n - 1)
+                    def _(g=g, n=n):
+                        y_copy(g, n).start()
 
         tab_copy(first + DEPTH - 1, 0).start()
         tab_copy(first + DEPTH - 1, 1).start()
@@ -335,15 +343,9 @@
         s_run[...] = total
 
     def absorb_body(k, carry):
-        y_copy(k).wait_recv()
         absorb(k, CHUNK)
         tx_copy(k).wait_send()
         tx_copy(n_chunks + k).wait_send()
-
-        @pl.when(k > 0)
-        def _():
-            y_copy(k - 1).wait_send()
-
         return carry
 
     y_tail_copy().wait_recv()
@@ -356,7 +358,9 @@
     all_of(stat2_slots, stat2_send, 3).wait()
     for dz in range(1, n_vp):
         pick_copy(dz).wait_send()
-    lax.fori_loop(0, n_full, absorb_body, 0)
+    for g, n in groups:
+        y_copy(g, n).wait_recv()
+        lax.fori_loop(g, g + n, absorb_body, 0)
 
     m_t = m_run[...].T
     top = jnp.max(m_t, axis=0, keepdims=True)
@@ -374,7 +378,8 @@
     for dz, dt, j in peers:
         lse_copy(dz, dt, j).start()
 
-    y_copy(n_full - 1).wait_send()
+    for g, n in groups:
+        y_copy(g, n).wait_send()
     all_of(lse_slots, lse_recv, len(peers)).wait()
     pairs = lse_slots[:, 0, :]
     top = jnp.max(pairs, axis=0, keepdims=True)
@@ -419,7 +424,7 @@
         n_full, rem = divmod(seg, CHUNK)
         n_chunks = n_full + 1
         rem_pad = -(-rem // LANES) * LANES
-        assert 2 * rows == LANES and n_vp == 4 and rem == 2 * LANES + LANES // 2 and n_full > DEPTH
+        assert 2 * rows == LANES and n_vp == 4 and rem == 2 * LANES + LANES // 2 and n_full >= 8
         f32, bf16 = jnp.float32, jnp.bfloat16
         dma = pltpu.SemaphoreType.DMA
         hbm = pl.BlockSpec(memory_space=pltpu.HBM)

time: 108 us -> 108 us (level)
  no operation moved by 1% of the time
where the time goes in v7:
time: 108 us
  Pallas kernels  107 us (99%)
    pallas_call x1, Pallas kernels, per_device(): pl.pallas_call(functools.partial(head_kernel, n_vp, n_full, rem, width),...  105 us
    pallas_call x1, Pallas kernels, per_device(): pl.pallas_call(functools.partial(finish_kernel, n_full, rem), out_shape=(...  2.2 us

profile of v7, /device:TPU:0, one launch (start us, length us, event | category | flops | bytes accessed | tf_op | source)
XLA Modules:
  0.0 107.5 jit_solution(6240607711528325877)
XLA Ops:
  0.6 104.7 %head.1 = (f32[21,64,768]{2,1,0:T(8,128)S(1)}, f32[8,128]{1,0:T(8,128)S(1)}, bf16[64,384]{1,0:T(8,128)(2,1)S(1)}) custom-call(bf16[64,384]{1,0:T(8,128)(2,1)} %hid_hbm.1, f32[384]{0:T(512)} %gain1_hbm.1, f32[384]{0:T(512)} %bias1_hbm.1, bf16[62720,384]{1,0:T(8,128)(2,1)} %tab_hbm.1, s32[1,64]{1,0:T(1,128)} %bitcast.2, f32[384]{0:T(512)} %gain2_hbm.1, ...), custom_call_target="tpu_custom_call" | custom-call | tf_op jit(solution)/shard_map/head/pallas_call | solution.py:432
  105.3 2.2 %finish.1 = (f32[64,15680]{1,0:T(8,128)}, f32[1,64]{1,0:T(1,128)}, bf16[64,384]{1,0:T(8,128)(2,1)}) custom-call(f32[21,64,768]{2,1,0:T(8,128)S(1)} %get-tuple-element.9.logits, f32[8,128]{1,0:T(8,128)S(1)} %get-tuple-element.10.lse, bf16[64,384]{1,0:T(8,128)(2,1)S(1)} %get-tuple-element.11.next_rows), custom_call_target="tpu_custom_call" | custom-call | tf_op jit(solution)/shard_map/finish/pallas_call | solution.py:478

commit v8 on v7

--- a/solution.py
+++ b/solution.py
@@ -8,7 +8,7 @@
 from jax.sharding import PartitionSpec as P
 
 NORM_EPS = 1e-5
-CHUNK = 768
+CHUNK = 1536
 LANES = 128
 DEPTH = 3
 LOWEST = -3.0e38

time: 108 us -> 107 us (level)
  no operation moved by 1% of the time
where the time goes in v8:
time: 107 us
  Pallas kernels  106 us (99%)
    pallas_call x1, Pallas kernels, per_device(): pl.pallas_call(functools.partial(head_kernel, n_vp, n_full, rem, width),...  104 us
    pallas_call x1, Pallas kernels, per_device(): pl.pallas_call(functools.partial(finish_kernel, n_full, rem), out_shape=(...  2.2 us

profile of v8, /device:TPU:0, one launch (start us, length us, event | category | flops | bytes accessed | tf_op | source)
XLA Modules:
  0.0 106.9 jit_solution(4229709764296431845)
XLA Ops:
  0.6 104.1 %head.1 = (f32[11,64,1536]{2,1,0:T(8,128)S(1)}, f32[8,128]{1,0:T(8,128)S(1)}, bf16[64,384]{1,0:T(8,128)(2,1)S(1)}) custom-call(bf16[64,384]{1,0:T(8,128)(2,1)} %hid_hbm.1, f32[384]{0:T(512)} %gain1_hbm.1, f32[384]{0:T(512)} %bias1_hbm.1, bf16[62720,384]{1,0:T(8,128)(2,1)} %tab_hbm.1, s32[1,64]{1,0:T(1,128)} %bitcast.2, f32[384]{0:T(512)} %gain2_hbm.1, ...), custom_call_target="tpu_custom_call" | custom-call | tf_op jit(solution)/shard_map/head/pallas_call | solution.py:432
  104.7 2.2 %finish.1 = (f32[64,15680]{1,0:T(8,128)}, f32[1,64]{1,0:T(1,128)}, bf16[64,384]{1,0:T(8,128)(2,1)}) custom-call(f32[11,64,1536]{2,1,0:T(8,128)S(1)} %get-tuple-element.9.logits, f32[8,128]{1,0:T(8,128)S(1)} %get-tuple-element.10.lse, bf16[64,384]{1,0:T(8,128)(2,1)S(1)} %get-tuple-element.11.next_rows), custom_call_target="tpu_custom_call" | custom-call | tf_op jit(solution)/shard_map/finish/pallas_call | solution.py:478

commit v9 on v6

--- a/solution.py
+++ b/solution.py
@@ -8,7 +8,7 @@
 from jax.sharding import PartitionSpec as P
 
 NORM_EPS = 1e-5
-CHUNK = 768
+CHUNK = 2560
 LANES = 128
 DEPTH = 3
 LOWEST = -3.0e38
@@ -165,9 +165,20 @@
             device_id={"tp": sibling}, device_id_type=MESH,
         )
 
+    cut = CHUNK // 4 * 3
+
     def y_copy(e):
         return pltpu.make_async_remote_copy(
             src_ref=acc.at[e], dst_ref=y_rx.at[e], send_sem=y_send.at[e], recv_sem=y_recv.at[e],
+            device_id={"tp": across}, device_id_type=MESH,
+        )
+
+    def y_last(part):
+        at = pl.ds(0, cut) if part == 0 else pl.ds(cut, CHUNK - cut)
+        sem = (n_full - 1) if part == 0 else n_chunks
+        return pltpu.make_async_remote_copy(
+            src_ref=acc.at[n_full - 1, :, at], dst_ref=y_rx.at[n_full - 1, :, at],
+            send_sem=y_send.at[sem], recv_sem=y_recv.at[sem],
             device_id={"tp": across}, device_id_type=MESH,
         )
 
@@ -244,11 +255,14 @@
         else:
             acc[last, :, 0:rem_pad] = acc[last, :, 0:rem_pad] + rx[last, :, 0:rem_pad]
 
-        def finish(e):
+        def finish(e, end=False):
             tx_copy(e).wait_recv()
             acc[e] = acc[e] + rx[e]
-            if phase == 0:
+            if phase == 0 and not end:
                 y_copy(e).start()
+            elif phase == 0:
+                y_last(0).start()
+                y_last(1).start()
 
         tab_copy(first + DEPTH - 1, 0).start()
         tab_copy(first + DEPTH - 1, 1).start()
@@ -283,7 +297,7 @@
             return carry
 
         lax.fori_loop(first + 1, first + n_full, body, 0)
-        finish(last - 1)
+        finish(last - 1, end=True)
 
     signal_vp(near_sem.at[0])
     run_phase(0)
@@ -314,21 +328,21 @@
         x2, stat2_slots, stat2_send, stat2_recv, gain2[...].reshape(1, width), bias2[...].reshape(1, width)
     ).astype(jnp.bfloat16)
 
-    def absorb(k, cols):
+    def absorb(k, cols, skip=0):
         e = n_chunks + k
-        blocks = cols // LANES
+        blocks = range(skip // LANES, cols // LANES)
         top = m_run[...]
-        for b in range(blocks):
+        for b in blocks:
             sl = pl.ds(b * LANES, LANES)
-            z = acc[e, :, sl] + (y_rx[k, :, sl] if cols == CHUNK else tail_block(b))
+            z = acc[e, :, sl] + (tail_block(b) if k is n_full else y_rx[k, :, sl])
             logits[k, :, sl] = z
-            if cols != CHUNK and (b + 1) * LANES > rem:
+            if k is n_full and (b + 1) * LANES > rem:
                 z = jnp.where(lane < rem - b * LANES, z, -jnp.inf)
             top = jnp.maximum(top, z)
         total = s_run[...] * jnp.exp(m_run[...] - top)
-        for b in range(blocks):
+        for b in blocks:
             z = logits[k, :, pl.ds(b * LANES, LANES)]
-            if cols != CHUNK and (b + 1) * LANES > rem:
+            if k is n_full and (b + 1) * LANES > rem:
                 z = jnp.where(lane < rem - b * LANES, z, -jnp.inf)
             total = total + jnp.exp(z - top)
         m_run[...] = top
@@ -339,11 +353,6 @@
         absorb(k, CHUNK)
         tx_copy(k).wait_send()
         tx_copy(n_chunks + k).wait_send()
-
-        @pl.when(k > 0)
-        def _():
-            y_copy(k - 1).wait_send()
-
         return carry
 
     y_tail_copy().wait_recv()
@@ -356,7 +365,13 @@
     all_of(stat2_slots, stat2_send, 3).wait()
     for dz in range(1, n_vp):
         pick_copy(dz).wait_send()
-    lax.fori_loop(0, n_full, absorb_body, 0)
+    lax.fori_loop(0, n_full - 1, absorb_body, 0)
+    tx_copy(n_full - 1).wait_send()
+    tx_copy(n_chunks + n_full - 1).wait_send()
+    y_last(0).wait_recv()
+    absorb(n_full - 1, cut)
+    y_last(1).wait_recv()
+    absorb(n_full - 1, CHUNK, cut)
 
     m_t = m_run[...].T
     top = jnp.max(m_t, axis=0, keepdims=True)
@@ -374,7 +389,10 @@
     for dz, dt, j in peers:
         lse_copy(dz, dt, j).start()
 
-    y_copy(n_full - 1).wait_send()
+    for e in range(n_full - 1):
+        y_copy(e).wait_send()
+    y_last(0).wait_send()
+    y_last(1).wait_send()
     all_of(lse_slots, lse_recv, len(peers)).wait()
     pairs = lse_slots[:, 0, :]
     top = jnp.max(pairs, axis=0, keepdims=True)
@@ -454,7 +472,7 @@
                 dma((6,)), dma((DEPTH, 2)), dma((4,)),
                 dma((1,)), dma((1,)), dma((1,)), dma((1,)),
                 dma((2 * n_chunks,)), dma((2 * n_chunks,)),
-                dma((n_chunks,)), dma((n_chunks,)),
+                dma((n_chunks + 1,)), dma((n_chunks + 1,)),
                 dma((n_vp - 1,)), dma((n_vp - 1,)),
                 dma((1,)), dma((1,)),
                 pltpu.SemaphoreType.REGULAR((3,)),

time: 108 us -> 107 us (level)
  no operation moved by 1% of the time
where the time goes in v9:
time: 107 us
  Pallas kernels  107 us (100%)
    pallas_call x1, Pallas kernels, per_device(): pl.pallas_call(functools.partial(head_kernel, n_vp, n_full, rem, width),...  104 us
    pallas_call x1, Pallas kernels, per_device(): pl.pallas_call(functools.partial(finish_kernel, n_full, rem), out_shape=(...  2.2 us

profile of v9, /device:TPU:0, one launch (start us, length us, event | category | flops | bytes accessed | tf_op | source)
XLA Modules:
  0.0 107.2 jit_solution(732399910688908207)
XLA Ops:
  0.6 104.4 %head.1 = (f32[7,64,2560]{2,1,0:T(8,128)S(1)}, f32[8,128]{1,0:T(8,128)S(1)}, bf16[64,384]{1,0:T(8,128)(2,1)S(1)}) custom-call(bf16[64,384]{1,0:T(8,128)(2,1)} %hid_hbm.1, f32[384]{0:T(512)} %gain1_hbm.1, f32[384]{0:T(512)} %bias1_hbm.1, bf16[62720,384]{1,0:T(8,128)(2,1)} %tab_hbm.1, s32[1,64]{1,0:T(1,128)} %bitcast.2, f32[384]{0:T(512)} %gain2_hbm.1, ...), custom_call_target="tpu_custom_call" | custom-call | tf_op jit(solution)/shard_map/head/pallas_call | solution.py:445
  105.0 2.2 %finish.1 = (f32[64,15680]{1,0:T(8,128)}, f32[1,64]{1,0:T(1,128)}, bf16[64,384]{1,0:T(8,128)(2,1)}) custom-call(f32[7,64,2560]{2,1,0:T(8,128)S(1)} %get-tuple-element.9.logits, f32[8,128]{1,0:T(8,128)S(1)} %get-tuple-element.10.lse, bf16[64,384]{1,0:T(8,128)(2,1)S(1)} %get-tuple-element.11.next_rows), custom_call_target="tpu_custom_call" | custom-call | tf_op jit(solution)/shard_map/finish/pallas_call | solution.py:491

commit v10 on v9

--- a/solution.py
+++ b/solution.py
@@ -8,7 +8,7 @@
 from jax.sharding import PartitionSpec as P
 
 NORM_EPS = 1e-5
-CHUNK = 2560
+CHUNK = 1536
 LANES = 128
 DEPTH = 3
 LOWEST = -3.0e38

time: 107 us -> 107 us (level)
  no operation moved by 1% of the time
where the time goes in v10:
time: 107 us
  Pallas kernels  106 us (99%)
    pallas_call x1, Pallas kernels, per_device(): pl.pallas_call(functools.partial(head_kernel, n_vp, n_full, rem, width),...  104 us
    pallas_call x1, Pallas kernels, per_device(): pl.pallas_call(functools.partial(finish_kernel, n_full, rem), out_shape=(...  2.2 us

profile of v10, /device:TPU:0, one launch (start us, length us, event | category | flops | bytes accessed | tf_op | source)
XLA Modules:
  0.0 107.0 jit_solution(15556359375585801214)
XLA Ops:
  0.6 104.1 %head.1 = (f32[11,64,1536]{2,1,0:T(8,128)S(1)}, f32[8,128]{1,0:T(8,128)S(1)}, bf16[64,384]{1,0:T(8,128)(2,1)S(1)}) custom-call(bf16[64,384]{1,0:T(8,128)(2,1)} %hid_hbm.1, f32[384]{0:T(512)} %gain1_hbm.1, f32[384]{0:T(512)} %bias1_hbm.1, bf16[62720,384]{1,0:T(8,128)(2,1)} %tab_hbm.1, s32[1,64]{1,0:T(1,128)} %bitcast.2, f32[384]{0:T(512)} %gain2_hbm.1, ...), custom_call_target="tpu_custom_call" | custom-call | tf_op jit(solution)/shard_map/head/pallas_call | solution.py:445
  104.8 2.2 %finish.1 = (f32[64,15680]{1,0:T(8,128)}, f32[1,64]{1,0:T(1,128)}, bf16[64,384]{1,0:T(8,128)(2,1)}) custom-call(f32[11,64,1536]{2,1,0:T(8,128)S(1)} %get-tuple-element.9.logits, f32[8,128]{1,0:T(8,128)S(1)} %get-tuple-element.10.lse, bf16[64,384]{1,0:T(8,128)(2,1)S(1)} %get-tuple-element.11.next_rows), custom_call_target="tpu_custom_call" | custom-call | tf_op jit(solution)/shard_map/finish/pallas_call | solution.py:491

commit v11 on v8

--- a/solution.py
+++ b/solution.py
@@ -37,8 +37,8 @@
     my_rank = vp * 4 + tp
 
     peers = []
-    for dz in reversed(range(n_vp)):
-        for dt in reversed(range(4)):
+    for dz in (*range(1, n_vp), 0):
+        for dt in (2, 1, 3, 0):
             if dz or dt:
                 peers.append((dz, dt, dz * 4 + dt))
 

time: 107 us -> 107 us (level)
  no operation moved by 1% of the time
where the time goes in v11:
time: 107 us
  Pallas kernels  106 us (99%)
    pallas_call x1, Pallas kernels, per_device(): pl.pallas_call(functools.partial(head_kernel, n_vp, n_full, rem, width),...  104 us
    pallas_call x1, Pallas kernels, per_device(): pl.pallas_call(functools.partial(finish_kernel, n_full, rem), out_shape=(...  2.2 us

profile of v11, /device:TPU:0, one launch (start us, length us, event | category | flops | bytes accessed | tf_op | source)
XLA Modules:
  0.0 106.8 jit_solution(431934947903032252)
XLA Ops:
  0.6 104.0 %head.1 = (f32[11,64,1536]{2,1,0:T(8,128)S(1)}, f32[8,128]{1,0:T(8,128)S(1)}, bf16[64,384]{1,0:T(8,128)(2,1)S(1)}) custom-call(bf16[64,384]{1,0:T(8,128)(2,1)} %hid_hbm.1, f32[384]{0:T(512)} %gain1_hbm.1, f32[384]{0:T(512)} %bias1_hbm.1, bf16[62720,384]{1,0:T(8,128)(2,1)} %tab_hbm.1, s32[1,64]{1,0:T(1,128)} %bitcast.2, f32[384]{0:T(512)} %gain2_hbm.1, ...), custom_call_target="tpu_custom_call" | custom-call | tf_op jit(solution)/shard_map/head/pallas_call | solution.py:432
  104.6 2.2 %finish.1 = (f32[64,15680]{1,0:T(8,128)}, f32[1,64]{1,0:T(1,128)}, bf16[64,384]{1,0:T(8,128)(2,1)}) custom-call(f32[11,64,1536]{2,1,0:T(8,128)S(1)} %get-tuple-element.9.logits, f32[8,128]{1,0:T(8,128)S(1)} %get-tuple-element.10.lse, bf16[64,384]{1,0:T(8,128)(2,1)S(1)} %get-tuple-element.11.next_rows), custom_call_target="tpu_custom_call" | custom-call | tf_op jit(solution)/shard_map/finish/pallas_call | solution.py:478
